TPU v7x, 256 devices: a whole 4x4x8 slice. The times are simulated.
256 devices in a mesh: tok: 32 (over y, z), voc: 8 (over x, core).
Axes of the slice: x: 4, y: 4, z: 8, core: 2. Of those that a mesh axis runs over, the one named last changes fastest.
Arguments:
- hidden: bfloat16 [768, 4096], P(('tok', 'voc'))
- head_weight: bfloat16 [4096, 128256], P(None, ('tok', 'voc'))
- actions: int32 [768], P(('tok', 'voc')), may hold values from 0 to 128255
- old_logp: bfloat16 [768], P(('tok', 'voc')), may hold values from -80 to 1
- advantage: bfloat16 [768], P(('tok', 'voc')), may hold values from -4 to 4
- loss_mask: int32 [768], P(('tok', 'voc')), may hold values 0 or 1
Outputs:
- grad_weight: bfloat16 [4096, 128256], P(None, ('tok', 'voc'))
- grad_hidden: float32 [768, 4096], P(('tok', 'voc'))
All inputs are finite; a program needn't handle non-finite values. No bound on the sum of `loss_mask` on one device may be relied on, other than what follows from the above.
Results may differ from a plain program's by a relative error of at most 0.0047.
Values may be sent and summed in bfloat16 or wider, within the bound.
No kernel may reach another device: no remote copies, remote signals or barrier semaphores. Data moves between devices by JAX's collectives and lax.ppermute only.
A program may use at most 128 MiB of HBM per device.

v0:
```python
import jax
import jax.numpy as jnp
from jax import lax
from jax.sharding import Mesh
from jax.sharding import PartitionSpec as P

TOK_VOC = ("tok_0", "tok_1", "voc_0", "voc_1")


def in_one_piece(arrays, axis, dim, along):
    columns = [a.reshape(*a.shape[:along], -1) for a in arrays]
    both = jnp.concatenate(columns, axis=along)
    whole, at, outs = (lax.all_gather(both, axis, axis=dim, tiled=True), 0, [])
    for a, column in zip(arrays, columns):
        piece = whole[..., at : at + column.shape[along]]
        outs.append(piece.reshape(*piece.shape[:along], *a.shape[along:]))
        at += column.shape[along]
    return tuple(outs)


def turned_gather(arrays, axis, dims):
    turned = [jnp.moveaxis(a, dim, 0) for a, dim in zip(arrays, dims)]
    widths = [t[0].size for t in turned]
    both = jnp.concatenate([t.reshape(-1, w) for t, w in zip(turned, widths)], axis=1)
    whole = lax.all_gather(both, axis, axis=0, tiled=True)
    blocks = jnp.split(whole, [sum(widths[:k]) for k in range(1, len(widths))], axis=1)
    return tuple(
        (
            jnp.moveaxis(b.reshape(-1, *t.shape[1:]), 0, dim)
            for b, t, dim in zip(blocks, turned, dims)
        )
    )


def all_in_one(value, axis):
    leaves = jax.tree.leaves(value)
    sequence = sorted(range(len(leaves)), key=lambda k: -leaves[k].size)
    width = (1, *leaves[sequence[0]].shape)[-1]
    lines = [
        jnp.pad(leaves[k].reshape(-1), (0, -leaves[k].size % width)).reshape(-1, width)
        for k in sequence
    ]
    both, at, found = (lax.all_gather(jnp.concatenate(lines), axis), 0, {})
    for k, line in zip(sequence, lines):
        piece = both[:, at : at + len(line)].reshape(len(both), -1)
        found[k] = piece[:, : leaves[k].size].reshape(-1, *leaves[k].shape)
        at += len(line)
    numbers = iter(range(len(leaves)))
    return jax.tree.map(lambda _: found[next(numbers)], value)


def combined_by_axis(value, axes, combine):
    for axis in axes:
        pieces = all_in_one(value, axis)
        value = jax.tree.map(lambda part: part[0], pieces)
        for k in range(1, lax.axis_size(axis)):
            value = combine(value, jax.tree.map(lambda part: part[k], pieces))
    return value


def combine_stats(first, second):
    top_a, sum_a, moment_a, target_a = first
    top_b, sum_b, moment_b, target_b = second
    top = jnp.maximum(top_a, top_b)
    scale_a = jnp.exp(top_a - top)
    scale_b = jnp.exp(top_b - top)
    return (
        top,
        sum_a * scale_a + sum_b * scale_b,
        moment_a * scale_a + moment_b * scale_b,
        target_a + target_b,
    )


def per_device(hidden, head_weight, actions, old_logp, advantage, loss_mask):
    hidden_all, old_all, advant_all = in_one_piece((hidden, old_logp, advantage), TOK_VOC, 0, 1)
    action_all, mask_all = turned_gather((actions, loss_mask), TOK_VOC, (0, 0))
    width = head_weight.shape[1]
    logits = jnp.dot(hidden_all, head_weight, preferred_element_type=jnp.float32)
    first_col = lax.axis_index(TOK_VOC) * width
    columns = first_col + lax.broadcasted_iota(jnp.int32, logits.shape, 1)
    matches = columns == action_all[:, None]
    target_part = jnp.sum(jnp.where(matches, logits, 0.0), axis=1)
    local_top = jnp.max(logits, axis=1)
    shifted = jnp.exp(logits - local_top[:, None])
    top, sumexp, moment, target = combined_by_axis(
        (local_top, jnp.sum(shifted, axis=1), jnp.sum(shifted * logits, axis=1), target_part),
        TOK_VOC,
        combine_stats,
    )
    lse = top + jnp.log(sumexp)
    mean_logit = moment / sumexp
    advant = advant_all.astype(jnp.float32)
    ratio = jnp.exp(target - lse - old_all.astype(jnp.float32))
    clipped = (advant > 0.0) & (ratio > 1.2) | (advant < 0.0) & (ratio < 0.8)
    active = jnp.where(clipped, 0.0, 1.0).astype(jnp.float32)
    weights = mask_all.astype(jnp.float32)
    policy = -advant * ratio * active * weights
    probability = jnp.exp(logits - lse[:, None])
    onehot = matches.astype(jnp.float32)
    dlogits = policy[:, None] * (onehot - probability) + 0.05 * weights[:, None] * probability * (
        logits - mean_logit[:, None]
    )
    dlogits = dlogits.astype(jnp.bfloat16)
    grad_hidden = lax.psum_scatter(
        lax.dot_general(
            dlogits, head_weight, (((1,), (1,)), ((), ())), preferred_element_type=jnp.float32
        ),
        TOK_VOC,
        scatter_dimension=0,
        tiled=True,
    )
    grad_weight = lax.dot_general(
        hidden_all, dlogits, (((0,), (0,)), ((), ())), preferred_element_type=jnp.float32
    ).astype(jnp.bfloat16)
    return (grad_weight, grad_hidden)


def solution(mesh):
    torus = Mesh(mesh.devices.reshape(4, 8, 4, 2), ("tok_0", "tok_1", "voc_0", "voc_1"))
    placed = (P(TOK_VOC, None), P(None, TOK_VOC), P(TOK_VOC), P(TOK_VOC), P(TOK_VOC), P(TOK_VOC))
    return jax.shard_map(
        per_device,
        mesh=torus,
        in_specs=placed,
        out_specs=(P(None, TOK_VOC), P(TOK_VOC, None)),
        check_vma=False,
    )
```

profile of v0, /device:TPU:8, one launch (start us, length us, event | category | flops | bytes accessed | tf_op | source)
XLA Modules:
  0.0 510.3 jit_solution(7638955065350822240)
XLA Ops:
  7.2 0.8 copy.32
  8.0 0.8 copy.33
  8.7 1.5 concatenate.18
  10.3 0.7 add_bitcast_fusion
  10.9 65.1 %all-gather.5 = s32[256,3,2]{1,2,0:T(2,128)S(1)} all-gather(s32[1,3,2]{1,2,0:T(2,128)S(1)} %add_bitcast_fusion), channel_id=1, replica_groups=mesh['tok_0'=4,'tok_1'=8,'voc_0'=4,'voc_1'=2] {'tok_0','tok_1','voc_0','..., dimensions={0}, use_global_device_ids=true | all-gather | bytes 6168 | tf_op jit(solution)/shard_map/all_gather | solution.py:25
  76.0 0.2 reshape.1556
  76.3 56.5 %all-gather.12.cloned.1.call-done = bf16[256,3,4098]{2,1,0:T(4,128)(2,1)} async-done(((bf16[1,3,4098]{2,1,0:T(4,128)(2,1)}), bf16[256,3,4098]{2,1,0:T(4,128)(2,1)}) %all-gather.12.cloned.1.call-update) | async-done | bytes 6294544 | tf_op jit(solution)/shard_map/all_gather | solution.py:13
  132.8 13.9 %reshape.1554 = bf16[768,4098]{1,0:T(8,128)(2,1)} reshape(bf16[256,3,4098]{2,1,0:T(4,128)(2,1)} %all-gather.12.cloned.1.call-done) | data formatting | bytes 12589056
  146.7 7.4 %fusion.122 = (f32[768]{0:T(1024)S(1)}, f32[768,501]{0,1:T(8,128)S(1)}) fusion(bf16[4096,501]{0,1:T(8,128)(2,1)} %param.7, bf16[768,4098]{1,0:T(8,128)(2,1)} %reshape.1554), kind=kOutput, calls=%fused_computation.235 | convolution fusion | flops 3152403456 | bytes 11962368 | tf_op jit(solution)/shard_map/dot_general | solution.py:79
  154.1 0.5 fusion.8
  154.7 12.1 %all-gather.6 = f32[4,4,768]{2,1,0:T(4,128)S(1)} all-gather(f32[1,4,768]{2,1,0:T(4,128)S(1)} %maximum_bitcast_fusion), channel_id=2, replica_groups=mesh['tok_0'=4,'tok_1'=8,'voc_0'=4,'voc_1'=2] {'tok_0'}, dimensions={0}, use_global_device_ids=true | all-gather | bytes 61440 | tf_op jit(solution)/shard_map/all_gather | solution.py:43
  167.0 24.6 %all-gather.7 = f32[8,4,768]{2,1,0:T(4,128)S(1)} all-gather(f32[1,4,768]{2,1,0:T(4,128)S(1)} %maximum_bitcast_fusion.1), channel_id=3, replica_groups=mesh['tok_0'=4,'tok_1'=8,'voc_0'=4,'voc_1'=2] {'tok_1'}, dimensions={0}, use_global_device_ids=true | all-gather | bytes 110592 | tf_op jit(solution)/shard_map/all_gather | solution.py:43
  191.6 0.1 fusion.55
  191.7 0.1 fusion.34
  191.8 11.9 %all-gather.8 = f32[4,4,768]{2,1,0:T(4,128)S(1)} all-gather(f32[1,4,768]{2,1,0:T(4,128)S(1)} %maximum_bitcast_fusion.2), channel_id=4, replica_groups=mesh['tok_0'=4,'tok_1'=8,'voc_0'=4,'voc_1'=2] {'voc_0'}, dimensions={0}, use_global_device_ids=true | all-gather | bytes 61440 | tf_op jit(solution)/shard_map/all_gather | solution.py:43
  203.8 1.2 fusion.121
  205.0 1.8 all-gather.9
  206.9 0.1 copy.37
  207.0 0.1 copy.38
  207.2 0.1 multiply_reduce_fusion.2
  207.3 9.0 %fusion.113 = f32[768,4096]{1,0:T(8,128)} fusion(bf16[4096,501]{0,1:T(8,128)(2,1)} %param.7, f32[768,501]{0,1:T(8,128)S(1)} %get-tuple-element.26, f32[768]{0:T(1024)S(1)} %get-tuple-element.24, f32[768]{0:T(1024)S(1)} %get-tuple-element.12, f32[768]{0:T(1024)S(1)} %get-tuple-element.23, f32[768]{0:T(1024)S(1)} %get-tuple-element.11, ...), kind=kOutput, calls=%fused_computation.233 | convolution fusion | flops 3155867136 | bytes 18243540 | tf_op jit(solution)/shard_map/dot_general | solution.py:106
  216.3 8.3 %convolution_convert_fusion = bf16[4096,501]{0,1:T(8,128)(2,1)} fusion(bf16[768,4098]{1,0:T(8,128)(2,1)} %reshape.1554, f32[768,501]{0,1:T(8,128)S(1)} %get-tuple-element.26, f32[768]{0:T(1024)S(1)} %get-tuple-element.24, f32[768]{0:T(1024)S(1)} %get-tuple-element.12, f32[768]{0:T(1024)S(1)} %get-tuple-element.23, f32[768]{0:T(1024)S(1)} %get-tuple-element.11, ...), kind=kOutput, calls=%fused_computation | convolution fusion | flops 3157919232 | bytes 11952084 | tf_op jit(solution)/shard_map/dot_general | solution.py:113
  224.6 277.2 %all-reduce.3.cloned.1.call-done = f32[768,4096]{1,0:T(8,128)} async-done(((f32[768,4096]{1,0:T(8,128)}), f32[768,4096]{1,0:T(8,128)}) %all-reduce.3.cloned.1.call-update) | async-done | bytes 12582928
  501.8 1.6 constant_dynamic-slice_fusion
  (24 shorter events, 0.5 us)
Async XLA Ops:
  7.2 125.6 %all-gather.12.cloned.1.call-start = ((), (), s32[]{:S(2)}) async-start(), calls=%async_computation | async-start | bytes 8684544 | tf_op jit(solution)/shard_map/all_gather | solution.py:13
  10.2 491.6 %all-reduce.3.cloned.1.call-start = ((), (), s32[]{:S(2)}) async-start(), calls=%async_computation.1 | async-start | bytes 25165824
Sparse Core Ops, SparseCore 0:
  12.2 120.5 all-gather.11
  216.4 285.3 all-reduce.2
where the time goes:
time: 511 us; the launch traced here: 510 us
  waiting for transfers between devices  334 us (65%)
  blocking collectives  116 us (23%)
  matrix products  24.7 us (5%)
  local copies, waits for them, and re-layouts  20.3 us (4%)
  between operations  14.2 us (3%)
    unnamed x3, waiting for transfers between devices  277 us
    all_gather x1, blocking collectives, turned_gather(): whole = lax.all_gather(both, axis, axis=0, tiled=True)  65.1 us
    all_gather x1, waiting for transfers between devices, in_one_piece(): whole, at, outs = (lax.all_gather(both, axis, axis=dim, tiled=True), 0, [])  56.5 us
    all_gather x4, blocking collectives, all_in_one(): both, at, found = (lax.all_gather(jnp.concatenate(lines), axis), 0, {})  50.5 us
    unnamed x5, local copies, waits for them, and re-layouts  16 us
  transfers between devices with their start and end apart: 2, of which 2 were waited for; matrix products, arithmetic and copies ran while one was open for 2% of the time, Pallas kernels for 0%

commit v1 on v0

v1 whole, which is shorter than its diff:
```python
import jax
import jax.numpy as jnp
from jax import lax
from jax.sharding import Mesh
from jax.sharding import PartitionSpec as P

Y, Z, X, C = "tok_0", "tok_1", "voc_0", "voc_1"
TOK_VOC = (Y, Z, X, C)
NY, NZ, NX, NC = 4, 8, 4, 2
EXTRA = 128


def place(y, z, x, c):
    return ((y % NY) * NZ + z % NZ) * NX * NC + (x % NX) * NC + c % NC


def along_y(core):
    return [[place(y, z, x, core) for y in range(NY)] for z in range(NZ) for x in range(NX)]


def along_x(core):
    return [[place(y, z, x, core) for x in range(NX)] for y in range(NY) for z in range(NZ)]


LONG = along_y(0) + along_x(1)
SHORT = along_x(0) + along_y(1)
SWAP = [
    (place(y, z, x, c), place(y, z, x, 1 - c))
    for y in range(NY)
    for z in range(NZ)
    for x in range(NX)
    for c in range(NC)
]


def exchange(blocks, axis, groups=None):
    return lax.all_to_all(blocks, axis, 0, 0, axis_index_groups=groups)


def gathered(block, count, axis, groups=None):
    whole = exchange(jnp.broadcast_to(block, (count, *block.shape)), axis, groups)
    return whole.reshape(-1, *block.shape[1:])


def scattered(partial, count, axis, groups=None):
    pieces = exchange(partial.reshape(count, -1, partial.shape[1]), axis, groups)
    return jnp.sum(pieces.astype(jnp.float32), axis=0)


def combined(stats, count, axis):
    pieces = exchange(jnp.broadcast_to(stats, (count, *stats.shape)), axis)
    top = jnp.max(pieces[:, 0], axis=0)
    scale = jnp.exp(pieces[:, 0] - top)
    return jnp.stack(
        [
            top,
            jnp.sum(pieces[:, 1] * scale, axis=0),
            jnp.sum(pieces[:, 2] * scale, axis=0),
            jnp.sum(pieces[:, 3], axis=0),
        ]
    )


def per_device(hidden, head_weight, actions, old_logp, advantage, loss_mask):
    model, width = head_weight.shape
    core = lax.axis_index(C)
    digits = [actions % 128, (actions // 128) % 128, actions // 16384, loss_mask]
    columns = [d.astype(jnp.bfloat16) for d in digits] + [old_logp, advantage]
    extra = jnp.pad(jnp.stack(columns, axis=1), ((0, 0), (0, EXTRA - len(columns))))
    own = jnp.concatenate([hidden, extra], axis=1)
    own = gathered(own, NZ, Z)
    own = gathered(own, 4, TOK_VOC, SHORT)
    own = gathered(own, 4, TOK_VOC, LONG)
    other = lax.ppermute(own, TOK_VOC, SWAP)
    half = own.shape[0]
    both = jnp.concatenate([own, other], axis=0)
    hidden_all = both[:, :model]
    small = both[:, model : model + 8].astype(jnp.float32)
    action_all = (small[:, 0] + 128.0 * small[:, 1] + 16384.0 * small[:, 2]).astype(jnp.int32)
    weights, old_all, advant = small[:, 3], small[:, 4], small[:, 5]

    logits = jnp.dot(hidden_all, head_weight, preferred_element_type=jnp.float32)
    first_col = lax.axis_index(TOK_VOC) * width
    columns = first_col + lax.broadcasted_iota(jnp.int32, logits.shape, 1)
    matches = columns == action_all[:, None]
    target_part = jnp.sum(jnp.where(matches, logits, 0.0), axis=1)
    local_top = jnp.max(logits, axis=1)
    shifted = jnp.exp(logits - local_top[:, None])
    stats = jnp.stack(
        [local_top, jnp.sum(shifted, axis=1), jnp.sum(shifted * logits, axis=1), target_part]
    )
    stats = combined(stats, NZ, Z)
    stats = combined(stats, NY, Y)
    turned = lambda s: jnp.where(core == 1, jnp.roll(s, half, axis=1), s)
    top, sumexp, moment, target = turned(combined(turned(stats), NX * NC, (X, C)))

    lse = top + jnp.log(sumexp)
    mean_logit = moment / sumexp
    ratio = jnp.exp(target - lse - old_all)
    clipped = (advant > 0.0) & (ratio > 1.2) | (advant < 0.0) & (ratio < 0.8)
    active = jnp.where(clipped, 0.0, 1.0).astype(jnp.float32)
    policy = -advant * ratio * active * weights
    probability = jnp.exp(logits - lse[:, None])
    onehot = matches.astype(jnp.float32)
    dlogits = policy[:, None] * (onehot - probability) + 0.05 * weights[:, None] * probability * (
        logits - mean_logit[:, None]
    )
    dlogits = dlogits.astype(jnp.bfloat16)

    def to_hidden(d):
        return lax.dot_general(
            d, head_weight, (((1,), (1,)), ((), ())), preferred_element_type=jnp.float32
        )

    theirs = lax.ppermute(to_hidden(dlogits[half:]).astype(jnp.bfloat16), TOK_VOC, SWAP)
    partial = (to_hidden(dlogits[:half]) + theirs.astype(jnp.float32)).astype(jnp.bfloat16)
    partial = scattered(partial, 4, TOK_VOC, LONG).astype(jnp.bfloat16)
    partial = scattered(partial, 4, TOK_VOC, SHORT).astype(jnp.bfloat16)
    grad_hidden = scattered(partial, NZ, Z)
    grad_weight = lax.dot_general(
        hidden_all, dlogits, (((0,), (0,)), ((), ())), preferred_element_type=jnp.float32
    ).astype(jnp.bfloat16)
    return (grad_weight, grad_hidden)


def solution(mesh):
    torus = Mesh(mesh.devices.reshape(NY, NZ, NX, NC), TOK_VOC)
    placed = (P(TOK_VOC, None), P(None, TOK_VOC), P(TOK_VOC), P(TOK_VOC), P(TOK_VOC), P(TOK_VOC))
    return jax.shard_map(
        per_device,
        mesh=torus,
        in_specs=placed,
        out_specs=(P(None, TOK_VOC), P(TOK_VOC, None)),
        check_vma=False,
    )
```

time: 511 us -> 186 us (0.36)
  waiting for transfers between devices: 334 us -> 19.7 us
  between operations: 14.2 us -> 1.02 us
  local copies, waits for them, and re-layouts: 20.3 us -> 9.71 us
  other arithmetic: 1.73 us -> 10.3 us
  starting transfers between devices: 0.08 us -> 8.29 us
  matrix products: 24.7 us -> 17.3 us
    unnamed x3 -> x0, waiting for transfers between devices: 277 us -> none
    all_to_all x0 -> x7, blocking collectives: none -> 119 us  [exchange(): return lax.all_to_all(blocks, axis, 0, 0, axis_index_groups=groups)]
    all_gather x5 -> x0, blocking collectives: 116 us -> none  [the longest x1 65.1 us: turned_gather(): whole = lax.all_gather(both, axis, axis=0, tiled=True)]
    all_gather x1 -> x0, waiting for transfers between devices: 56.5 us -> none  [in_one_piece(): whole, at, outs = (lax.all_gather(both, axis, axis=dim, tiled=True), 0, [])]
    unnamed x5 -> x9, local copies, waits for them, and re-layouts: 16 us -> 1.51 us
    ppermute x0 -> x2, waiting for transfers between devices: none -> 11.5 us  [the longest x1 5.89 us: per_device(): other = lax.ppermute(own, TOK_VOC, SWAP)]
    all_to_all x0 -> x2, waiting for transfers between devices: none -> 8.19 us  [exchange(): return lax.all_to_all(blocks, axis, 0, 0, axis_index_groups=groups)]
    all_to_all x0 -> x2, starting transfers between devices: none -> 8.1 us  [exchange(): return lax.all_to_all(blocks, axis, 0, 0, axis_index_groups=groups)]
  transfers between devices with their start and end apart: 2 -> 4, of which waited for: 2 -> 4; matrix products, arithmetic and copies ran while one was open for 2% -> 4% of each run, Pallas kernels for 0% -> 0%
where the time goes in v1:
time: 186 us; the launch traced here: 185 us
  blocking collectives  119 us (64%)
  waiting for transfers between devices  19.7 us (11%)
  matrix products  17.3 us (9%)
  other arithmetic  10.3 us (6%)
  local copies, waits for them, and re-layouts  9.71 us (5%)
  starting transfers between devices  8.29 us (4%)
    all_to_all x7, blocking collectives, exchange(): return lax.all_to_all(blocks, axis, 0, 0, axis_index_groups=groups)  119 us
    all_to_all x2, waiting for transfers between devices, exchange(): return lax.all_to_all(blocks, axis, 0, 0, axis_index_groups=groups)  8.19 us
    all_to_all x2, starting transfers between devices, exchange(): return lax.all_to_all(blocks, axis, 0, 0, axis_index_groups=groups)  8.1 us
    dot_general x1, matrix products, per_device(): jnp.dot(hidden_all, head_weight, preferred_element_type=jnp.float32)  6.99 us
    dot_general x1, matrix products, per_device(): lax.dot_general(hidden_all, dlogits, (((0,), (0,)), ((), ())), preferred_...  6.55 us
    ppermute x1, waiting for transfers between devices, per_device(): other = lax.ppermute(own, TOK_VOC, SWAP)  5.89 us
    ppermute x1, waiting for transfers between devices, per_device(): lax.ppermute(to_hidden(dlogits[half:]).astype(jnp.bfloat16), TOK_VOC, SWAP)  5.65 us
    reshape x2, local copies, waits for them, and re-layouts, gathered(): return whole.reshape(-1, *block.shape[1:])  5.6 us
  transfers between devices with their start and end apart: 4, of which 4 were waited for; matrix products, arithmetic and copies ran while one was open for 4% of the time, Pallas kernels for 0%

profile of v1, /device:TPU:8, one launch (start us, length us, event | category | flops | bytes accessed | tf_op | source)
XLA Modules:
  0.0 185.1 jit_solution(14749959666187470350)
XLA Ops:
  2.1 0.8 fusion.13
  3.0 20.3 %all_to_all.45 = bf16[8,3,4224]{2,1,0:T(4,128)(2,1)S(1)} all-to-all(bf16[8,3,4224]{2,1,0:T(4,128)(2,1)S(1)} %broadcast_in_dim.36), channel_id=1, replica_groups=mesh['tok_0'=4,'tok_1'=8,'voc_0'=4,'voc_1'=2] {'tok_1'}, dimensions={0} | all-to-all | bytes 405504 | tf_op jit(solution)/shard_map/all_to_all | solution.py:37
  23.5 13.7 %all_to_all.46 = bf16[4,24,4224]{2,1,0:T(8,128)(2,1)S(1)} all-to-all(bf16[4,24,4224]{2,1,0:T(8,128)(2,1)S(1)} %broadcast_in_dim.37), channel_id=1, replica_groups={{0,2,4,6},{8,10,12,14},{16,18,20,22},{24,26,28,30},{32,34,36,38},{40,42..., dimensions={0} | all-to-all | bytes 1622016 | tf_op jit(solution)/shard_map/all_to_all | solution.py:37
  37.5 26.0 %all_to_all.47 = bf16[4,96,4224]{2,1,0:T(8,128)(2,1)} all-to-all(bf16[4,96,4224]{2,1,0:T(8,128)(2,1)S(1)} %broadcast_in_dim.38), channel_id=1, replica_groups={{0,64,128,192},{2,66,130,194},{4,68,132,196},{6,70,134,198},{8,72,136,2..., dimensions={0} | all-to-all | bytes 6488064 | tf_op jit(solution)/shard_map/all_to_all | solution.py:37
  63.5 5.4 %copy.46 = bf16[384,4224]{0,1:T(8,128)(2,1)S(1)} copy(bf16[384,4224]{1,0:T(8,128)(2,1)} %bitcast.86) | data formatting | bytes 6488064 | tf_op jit(solution)/shard_map/reshape | solution.py:42
  69.0 5.9 %collective-permute-done = bf16[384,4224]{0,1:T(8,128)(2,1)} collective-permute-done((bf16[384,4224]{0,1:T(8,128)(2,1)S(1)}, bf16[384,4224]{0,1:T(8,128)(2,1)}, u32[]{:S(2)}, u32[]{:S(2)}) %collective-permute-start) | collective-permute-done | bytes 3244064 | tf_op jit(solution)/shard_map/ppermute | solution.py:74
  74.9 7.0 %fusion.55 = (f32[768]{0:T(1024)S(1)}, f32[768,501]{0,1:T(8,128)S(1)}) fusion(bf16[4096,501]{0,1:T(8,128)(2,1)} %param.7, bf16[384,4224]{0,1:T(8,128)(2,1)S(1)} %copy.46, bf16[384,4224]{0,1:T(8,128)(2,1)} %collective-permute-done), kind=kOutput, calls=%fused_computation.108 | convolution fusion | flops 3164986368 | bytes 12134400 | tf_op jit(solution)/shard_map/dot_general | solution.py:82
  82.0 0.9 fusion.35
  83.6 11.3 %all_to_all.48 = f32[8,4,768]{2,1,0:T(4,128)S(1)} all-to-all(f32[8,4,768]{2,1,0:T(4,128)S(1)} %broadcast_in_dim.40), channel_id=1, replica_groups=mesh['tok_0'=4,'tok_1'=8,'voc_0'=4,'voc_1'=2] {'tok_1'}, dimensions={0} | all-to-all | bytes 196608 | tf_op jit(solution)/shard_map/all_to_all | solution.py:37
  95.8 4.7 %all-to-all-start.4 = ((f32[4,4,768]{2,1,0:T(4,128)}), f32[4,4,768]{2,1,0:T(4,128)S(1)}, u32[]{:S(2)}, u32[]{:S(2)}) async-start(f32[4,4,768]{2,1,0:T(4,128)} %broadcast_in_dim.41), calls=%async_computation.4 | async-start | bytes 98304 | tf_op jit(solution)/shard_map/all_to_all | solution.py:37
  100.5 4.1 %all-to-all-done.4 = f32[4,4,768]{2,1,0:T(4,128)S(1)} async-done(((f32[4,4,768]{2,1,0:T(4,128)}), f32[4,4,768]{2,1,0:T(4,128)S(1)}, u32[]{:S(2)}, u32[]{:S(2)}) %all-to-all-start.4) | async-done | bytes 49184 | tf_op jit(solution)/shard_map/all_to_all | solution.py:37
  104.8 8.2 %all_to_all.49 = f32[8,4,768]{2,1,0:T(4,128)S(1)} all-to-all(f32[8,4,768]{2,1,0:T(4,128)S(1)} %broadcast_in_dim.42), channel_id=1, replica_groups=mesh['tok_0'=4,'tok_1'=8,'voc_0'=4,'voc_1'=2] {'voc_0','voc_1'}, dimensions={0} | all-to-all | bytes 196608 | tf_op jit(solution)/shard_map/all_to_all | solution.py:37
  113.3 0.9 fusion.40
  116.0 1.9 %convolution_convert_fusion.1 = bf16[384,4096]{1,0:T(8,128)(2,1)S(1)} fusion(bf16[4096,501]{0,1:T(8,128)(2,1)S(1)} %copy-done, bf16[768,501]{0,1:T(8,128)(2,1)S(1)} %fusion.5), kind=kOutput, calls=%fused_computation.5 | convolution fusion | flops 1577582592 | bytes 7661568 | tf_op jit(solution)/shard_map/dot_general | solution.py:111
  117.9 5.6 %collective-permute-done.1 = bf16[384,4096]{1,0:T(8,128)(2,1)S(1)} collective-permute-done((bf16[384,4096]{1,0:T(8,128)(2,1)S(1)}, bf16[384,4096]{1,0:T(8,128)(2,1)S(1)}, u32[]{:S(2)}, u32[]{:S(2)}) %collective-permute-start.1) | collective-permute-done | bytes 3145760 | tf_op jit(solution)/shard_map/ppermute | solution.py:115
  123.6 1.9 %add_convert_fusion = bf16[384,4096]{1,0:T(8,128)(2,1)S(1)} fusion(bf16[384,4096]{1,0:T(8,128)(2,1)S(1)} %collective-permute-done.1, bf16[4096,501]{0,1:T(8,128)(2,1)S(1)} %copy-done, bf16[768,501]{0,1:T(8,128)(2,1)S(1)} %fusion.5), kind=kOutput, calls=%fused_computation.3 | convolution fusion | flops 1580728320 | bytes 10807296 | tf_op jit(solution)/shard_map/dot_general | solution.py:111
  125.5 25.4 %all_to_all.50 = bf16[4,96,4096]{2,1,0:T(8,128)(2,1)} all-to-all(bf16[4,96,4096]{2,1,0:T(8,128)(2,1)S(1)} %bitcast.87), channel_id=1, replica_groups={{0,64,128,192},{2,66,130,194},{4,68,132,196},{6,70,134,198},{8,72,136,2..., dimensions={0} | all-to-all | bytes 6291456 | tf_op jit(solution)/shard_map/all_to_all | solution.py:37
  150.9 3.5 %reduce_sum.153 = bf16[96,4096]{1,0:T(8,128)(2,1)} reduce(bf16[4,96,4096]{2,1,0:T(8,128)(2,1)} %all_to_all.50, bf16[]{:T(256)} %constant.74.clone.1), dimensions={0}, to_apply=%region_16.17 | reduce | flops 1179648 | bytes 3932162 | tf_op jit(solution)/shard_map/reduce_sum | solution.py:47
  154.4 13.7 %all_to_all.51 = bf16[4,24,4096]{2,1,0:T(8,128)(2,1)} all-to-all(bf16[4,24,4096]{2,1,0:T(8,128)(2,1)} %bitcast.89), channel_id=1, replica_groups={{0,2,4,6},{8,10,12,14},{16,18,20,22},{24,26,28,30},{32,34,36,38},{40,42..., dimensions={0} | all-to-all | bytes 1572864 | tf_op jit(solution)/shard_map/all_to_all | solution.py:37
  168.2 1.3 reduce_sum.154
  169.5 0.8 reshape.82
  170.3 3.4 %all-to-all-start.8 = ((bf16[8,3,4096]{2,1,0:T(4,128)(2,1)}), bf16[8,3,4096]{2,1,0:T(4,128)(2,1)S(1)}, u32[]{:S(2)}, u32[]{:S(2)}) async-start(bf16[8,3,4096]{2,1,0:T(4,128)(2,1)} %reshape.82), calls=%async_computation.8 | async-start | bytes 524288 | tf_op jit(solution)/shard_map/all_to_all | solution.py:37
  173.7 6.6 %convolution_convert_fusion = bf16[4096,501]{0,1:T(8,128)(2,1)} fusion(bf16[768,501]{0,1:T(8,128)(2,1)} %copy-done.3, bf16[384,4224]{0,1:T(8,128)(2,1)S(1)} %copy.46, bf16[384,4224]{0,1:T(8,128)(2,1)} %collective-permute-done), kind=kOutput, calls=%fused_computation.4 | convolution fusion | flops 3166654464 | bytes 11361792 | tf_op jit(solution)/shard_map/dot_general | solution.py:120
  180.3 4.1 %all-to-all-done.8 = bf16[8,3,4096]{2,1,0:T(4,128)(2,1)S(1)} async-done(((bf16[8,3,4096]{2,1,0:T(4,128)(2,1)}), bf16[8,3,4096]{2,1,0:T(4,128)(2,1)S(1)}, u32[]{:S(2)}, u32[]{:S(2)}) %all-to-all-start.8) | async-done | bytes 196640 | tf_op jit(solution)/shard_map/all_to_all | solution.py:37
  (55 shorter events, 6.6 us)
Async XLA Ops:
  68.9 6.0 %collective-permute-start = (bf16[384,4224]{0,1:T(8,128)(2,1)S(1)}, bf16[384,4224]{0,1:T(8,128)(2,1)}, u32[]{:S(2)}, u32[]{:S(2)}) collective-permute-start(bf16[384,4224]{0,1:T(8,128)(2,1)S(1)} %copy.46), channel_id=1, source_target_pairs={{0,1},{1,0},{2,3},{3,2},{4,5},{5,4},{6,7},{7,6},{8,9},{9,8},{10,11... | collective-permute-start | bytes 9732104 | tf_op jit(solution)/shard_map/ppermute | solution.py:74
  81.9 1.1 copy-start.1
  95.8 8.8 %all-to-all-start.4 = ((f32[4,4,768]{2,1,0:T(4,128)}), f32[4,4,768]{2,1,0:T(4,128)S(1)}, u32[]{:S(2)}, u32[]{:S(2)}) async-start(f32[4,4,768]{2,1,0:T(4,128)} %broadcast_in_dim.41), calls=%async_computation.4 | async-start | bytes 98304 | tf_op jit(solution)/shard_map/all_to_all | solution.py:37
  113.3 1.4 copy-start.2
  113.3 2.7 %copy-start = (bf16[4096,501]{0,1:T(8,128)(2,1)S(1)}, bf16[4096,501]{0,1:T(8,128)(2,1)}, u32[]{:S(2)}) copy-start(bf16[4096,501]{0,1:T(8,128)(2,1)} %param.7) | copy-start | bytes 12312580
  116.0 7.6 %copy-start.3 = (bf16[768,501]{0,1:T(8,128)(2,1)}, bf16[768,501]{0,1:T(8,128)(2,1)S(1)}, u32[]{:S(2)}) copy-start(bf16[768,501]{0,1:T(8,128)(2,1)S(1)} %fusion.5) | copy-start | bytes 2308612
  117.8 5.7 %collective-permute-start.1 = (bf16[384,4096]{1,0:T(8,128)(2,1)S(1)}, bf16[384,4096]{1,0:T(8,128)(2,1)S(1)}, u32[]{:S(2)}, u32[]{:S(2)}) collective-permute-start(bf16[384,4096]{1,0:T(8,128)(2,1)S(1)} %convolution_convert_fusion.1), channel_id=1, source_target_pairs={{0,1},{1,0},{2,3},{3,2},{4,5},{5,4},{6,7},{7,6},{8,9},{9,8},{10,11... | collective-permute-start | bytes 9437192 | tf_op jit(solution)/shard_map/ppermute | solution.py:115
  170.3 14.1 %all-to-all-start.8 = ((bf16[8,3,4096]{2,1,0:T(4,128)(2,1)}), bf16[8,3,4096]{2,1,0:T(4,128)(2,1)S(1)}, u32[]{:S(2)}, u32[]{:S(2)}) async-start(bf16[8,3,4096]{2,1,0:T(4,128)(2,1)} %reshape.82), calls=%async_computation.8 | async-start | bytes 524288 | tf_op jit(solution)/shard_map/all_to_all | solution.py:37
